TPU v7x, 32 devices: a whole 2x2x4 slice. The times are simulated.
32 devices in a mesh: parts: 2 (over y), seq: 16 (over z, x, core).
Axes of the slice: x: 2, y: 2, z: 4, core: 2. Of those that a mesh axis runs over, the one named last changes fastest.
Arguments:
- queries: bfloat16 [8, 8192], P('parts', 'seq'), parts along dimension 0
- new_kv: bfloat16 [8, 2048], P('parts', 'seq'), parts along dimension 0, may hold values from -6 to 6
- keys: bfloat16 [64, 512, 1024], P(('parts', 'seq')), parts along dimension 0, may hold values from -6 to 6
- values: bfloat16 [64, 512, 1024], P(('parts', 'seq')), parts along dimension 0, may hold values from -6 to 6
- slot_request: int32 [64], P(('parts', 'seq')), parts along dimension 0, may hold values from 0 to 3, as said below
- slot_length: int32 [64], P(('parts', 'seq')), parts along dimension 0, may hold values from 1 to 512
Outputs:
- attended: bfloat16 [8, 8192], P('parts'), parts along dimension 0
There are 2 independent parts, one for each index of `parts`. A program takes and returns all parts, laid end to end along the dimension named above; each array names one. Nothing has to cross between parts.
Inputs may be any that keep to these rules, and one draw needn't show every extreme that they name: `slot_request`: every request number 0 to 3 owns at least one block.
All inputs are finite; a program needn't handle non-finite values.
Results may differ from a plain program's by a relative error of at most 0.0055.
Values may be sent and summed in bfloat16 or wider, within the bound.
A program may use at most 128 MiB of HBM per device.

v0:
```python
import jax
import jax.numpy as jnp
from jax import lax
from jax.sharding import PartitionSpec as P

H = 64
KVH = 8
DH = 128


very_negative = -1e30


def joined(x, axis, combine):
    everything = jax.tree.map(lambda part: lax.all_gather(part, axis), x)
    leading = jax.tree.map(lambda part: part[0], everything)

    def turn(k, so_far):
        return combine(so_far, jax.tree.map(lambda part: part[k], everything))

    return lax.fori_loop(1, lax.axis_size(axis), turn, leading)


def combine_parts(first, second):
    top_first, sum_first, out_first = first
    top_second, sum_second, out_second = second
    peak = jnp.maximum(top_first, top_second)
    weight_first = jnp.exp(top_first - peak)
    weight_second = jnp.exp(top_second - peak)
    summed = sum_first * weight_first + sum_second * weight_second
    outputs = out_first * weight_first[..., None] + out_second * weight_second[..., None]
    return (peak, summed, outputs)


def shards(queries, new_kv, keys, values, slot_request, slot_length):
    all_queries, all_new = (
        lax.all_gather(queries, "seq", axis=1, tiled=True),
        lax.all_gather(new_kv, "seq", axis=1, tiled=True),
    )
    requests = all_queries.shape[0]
    group_size = H // KVH
    score_scale = DH ** (-0.5)
    query_heads = all_queries.reshape(requests, KVH, group_size, DH)
    slot_count = keys.shape[0]
    block_len = keys.shape[1]
    owner = slot_request[:, None] == jnp.arange(requests, dtype=jnp.int32)[None, :]
    picked = jnp.einsum(
        "sr,rkgd->skgd", owner.astype(jnp.bfloat16), query_heads, preferred_element_type=jnp.float32
    ).astype(jnp.bfloat16)
    key_tiles = keys.reshape(slot_count, block_len, KVH, DH)
    value_tiles = values.reshape(slot_count, block_len, KVH, DH)
    scores = (
        jnp.einsum("skgd,stkd->skgt", picked, key_tiles, preferred_element_type=jnp.float32)
        * score_scale
    )
    inside = jnp.arange(block_len, dtype=jnp.int32)[None, :] < slot_length[:, None]
    scores = jnp.where(inside[:, None, None, :], scores, very_negative)
    slot_top = jnp.max(scores, axis=-1)
    weights = jnp.exp(scores - slot_top[..., None])
    slot_sum = jnp.sum(weights, axis=-1)
    slot_out = jnp.einsum(
        "skgt,stkd->skgd",
        weights.astype(jnp.bfloat16),
        value_tiles,
        preferred_element_type=jnp.float32,
    )
    owner_wide = owner[:, :, None, None]
    dense_top = jnp.max(jnp.where(owner_wide, slot_top[:, None], very_negative), axis=0)
    factor = jnp.where(owner_wide, jnp.exp(slot_top[:, None] - dense_top[None]), 0.0)
    dense_sum = jnp.sum(factor * slot_sum[:, None], axis=0)
    dense_out = jnp.einsum("srkg,skgd->rkgd", factor, slot_out, precision=lax.Precision.HIGHEST)
    total_top, total_sum, total_out = joined(
        (dense_top, dense_sum, dense_out), "seq", combine_parts
    )
    new_pair = all_new.astype(jnp.float32).reshape(requests, 2, KVH, DH)
    new_score = (
        jnp.einsum("rkgd,rkd->rkg", query_heads.astype(jnp.float32), new_pair[:, 0]) * score_scale
    )
    peak = jnp.maximum(total_top, new_score)
    old_weight = jnp.exp(total_top - peak)
    new_weight = jnp.exp(new_score - peak)
    rounded_new = new_weight.astype(jnp.bfloat16).astype(jnp.float32)
    numer = (
        total_out * old_weight[..., None] + rounded_new[..., None] * new_pair[:, 1][:, :, None, :]
    )
    denom = total_sum * old_weight + new_weight
    attended = numer / denom[..., None]
    return attended.reshape(requests, H * DH).astype(jnp.bfloat16)


def solution(mesh):
    placed = (
        P("parts", "seq"),
        P("parts", "seq"),
        P(("parts", "seq"), None, None),
        P(("parts", "seq"), None, None),
        P(("parts", "seq")),
        P(("parts", "seq")),
    )
    return jax.shard_map(
        shards, mesh=mesh, in_specs=placed, out_specs=P("parts", None), check_vma=False
    )
```

profile of v0, /device:TPU:0, one launch (start us, length us, event | category | flops | bytes accessed | tf_op | source)
XLA Modules:
  0.0 119.4 jit_solution(12509322590072242577)
XLA Ops:
  6.5 0.0 copy-start
  6.5 0.0 all-gather.5.cloned.1.call-start
  6.5 0.9 iota_compare_fusion.1
  7.4 0.7 iota_compare_fusion
  8.1 23.5 %all_gather.24 = bf16[4,8192]{1,0:T(4,128)(2,1)S(1)} all-gather(bf16[4,512]{1,0:T(4,128)(2,1)} %param.8), channel_id=1, replica_groups=mesh['parts'=2,'seq'=16] {'seq'}, dimensions={1}, use_global_device_ids=true | all-gather | bytes 69632 | tf_op jit(solution)/shard_map/all_gather | solution.py:37
  31.6 0.9 fusion.31
  32.5 0.0 copy-done
  32.5 0.7 fusion.35
  33.3 0.0 copy-start.1
  33.3 0.1 copy.14
  33.4 2.1 %fusion.3 = f32[2,8,8,128]{3,2,1,0:T(8,128)S(1)} fusion(f32[2,8,8,512]{3,2,1,0:T(8,128)S(1)} %get-tuple-element.217, f32[2,8,8]{2,1,0:T(8,128)S(1)} %get-tuple-element.216, bf16[2,512,1024]{2,1,0:T(8,128)(2,1)} %param.11), kind=kOutput, calls=%fused_computation.8 | convolution fusion | flops 16908288 | bytes 2425344 | tf_op jit(solution)/shard_map/skgt,stkd->skgd/dot_general | solution.py:61
  35.4 0.2 select_reduce_fusion
  35.6 0.9 convolution_bitcast_fusion
  36.5 0.7 copy.18
  37.2 0.0 all-gather.5.cloned.1.call-update
  37.2 0.1 copy.15
  37.3 0.0 copy-done.1
  37.3 17.5 %all_gather.31 = bf16[4,2048]{1,0:T(4,128)(2,1)S(1)} all-gather(bf16[4,128]{1,0:T(4,128)(2,1)S(1)} %copy-done.1), channel_id=1, replica_groups=mesh['parts'=2,'seq'=16] {'seq'}, dimensions={1}, use_global_device_ids=true | all-gather | bytes 17408 | tf_op jit(solution)/shard_map/all_gather | solution.py:38
  54.8 0.2 fusion.16
  55.0 0.1 copy.16
  55.1 0.2 multiply_reduce_fusion
  55.3 0.1 copy.17
  55.5 20.1 %all-gather = f32[64,8,8]{2,1,0:T(8,128)S(1)} all-gather(f32[4,8,8]{2,1,0:T(8,128)S(1)} %copy.15), channel_id=2, replica_groups=mesh['parts'=2,'seq'=16] {'seq'}, dimensions={0}, use_global_device_ids=true | all-gather | bytes 17408 | tf_op jit(solution)/shard_map/all_gather | solution.py:15
  75.5 18.1 %all-gather.1 = f32[64,8,8]{2,1,0:T(8,128)S(1)} all-gather(f32[4,8,8]{2,1,0:T(8,128)S(1)} %copy.17), channel_id=3, replica_groups=mesh['parts'=2,'seq'=16] {'seq'}, dimensions={0}, use_global_device_ids=true | all-gather | bytes 17408 | tf_op jit(solution)/shard_map/all_gather | solution.py:15
  93.7 0.1 fusion.19
  93.8 0.0 all-gather.5.cloned.1.call-done
  93.8 0.9 slice.26
  94.8 16.9 %while.19 = (s32[]{:T(128)}, f32[4,8,8]{2,1,0:T(8,128)S(1)}, f32[4,8,8]{2,1,0:T(8,128)S(1)}, f32[4,8,8,128]{3,2,1,0:T(8,128)S(1)}, f32[16,4,8,8]{3,2,1,0:T(8,128...) while((s32[]{:T(128)}, f32[4,8,8]{2,1,0:T(8,128)S(1)}, ...), condition=%wide.region_5.6_spmd, body=%wide.region_4.5_spmd.sunk | while | flops 99845 | bytes 403599 | solution.py:21
  94.8 1.1 fusion.42
  95.9 1.1 fusion.42
  97.1 1.1 fusion.42
  98.2 1.1 fusion.42
  99.3 1.1 fusion.42
  100.4 1.1 fusion.42
  101.6 1.1 fusion.42
  102.7 1.1 fusion.42
  103.8 1.1 fusion.42
  104.9 1.1 fusion.42
  106.1 1.1 fusion.42
  107.2 1.1 fusion.42
  108.3 1.1 fusion.42
  109.5 1.1 fusion.42
  110.6 1.1 fusion.42
  111.7 0.2 fusion.23
  111.9 0.7 copy.61
  (20 shorter events, 0.4 us)
Async XLA Ops:
  6.5 26.0 %copy-start = (bf16[2,512,1024]{2,1,0:T(8,128)(2,1)S(1)}, bf16[2,512,1024]{2,1,0:T(8,128)(2,1)}, u32[]{:S(2)}) copy-start(bf16[2,512,1024]{2,1,0:T(8,128)(2,1)} %param.10) | copy-start | bytes 6291460
  6.5 87.3 %all-gather.5.cloned.1.call-start = ((), (), s32[]{:S(2)}) async-start(), calls=%async_computation | async-start | bytes 2228224 | tf_op jit(solution)/shard_map/all_gather | solution.py:15
  33.3 4.1 %copy-start.1 = (bf16[4,128]{1,0:T(4,128)(2,1)S(1)}, bf16[4,128]{1,0:T(4,128)(2,1)}, u32[]{:S(2)}) copy-start(bf16[4,128]{1,0:T(4,128)(2,1)} %param.9) | copy-start | bytes 3076
Sparse Core Ops, SparseCore 0:
  37.3 39.2 all-gather.4
where the time goes:
time: 120 us; the launch traced here: 119 us
  blocking collectives  79.2 us (66%)
  other arithmetic  18.8 us (16%)
  between operations  13.5 us (11%)
  matrix products  4.7 us (4%)
  local copies, waits for them, and re-layouts  2.76 us (2%)
    all_gather x2, blocking collectives, joined(): everything = jax.tree.map(lambda part: lax.all_gather(part, axis), x)  38.2 us
    all_gather x1, blocking collectives, shards(): lax.all_gather(queries, 'seq', axis=1, tiled=True)  23.5 us
    all_gather x1, blocking collectives, shards(): lax.all_gather(new_kv, 'seq', axis=1, tiled=True)  17.5 us
    add x15, other arithmetic, combine_parts(): out_first * weight_first[..., None] + out_second * weight_second[..., None]  16.1 us
  transfers between devices with their start and end apart: 1, of which 0 were waited for; matrix products, arithmetic and copies ran while one was open for 1% of the time, Pallas kernels for 0%

commit v1 on v0

--- a/solution.py
+++ b/solution.py
@@ -1,14 +1,288 @@
+import functools
+import math
+
 import jax
 import jax.numpy as jnp
 from jax import lax
+from jax.experimental import pallas as pl
+from jax.experimental.pallas import tpu as pltpu
 from jax.sharding import PartitionSpec as P
 
 H = 64
 KVH = 8
 DH = 128
 
-
 very_negative = -1e30
+LOG2E = math.log2(math.e)
+GROUP = H // KVH
+
+
+def decode_kernel(
+    n,
+    request_ref,
+    length_ref,
+    q_ref,
+    new_ref,
+    keys_ref,
+    values_ref,
+    out_ref,
+    key_buf,
+    value_buf,
+    q_send,
+    q_buf,
+    new_buf,
+    part_send,
+    part_buf,
+    stat_send,
+    stat_buf,
+    out_send,
+    load_sem,
+    new_sem,
+    send_sem,
+    recv_sem,
+):
+    me = lax.axis_index("seq")
+    slots, block_len, _ = key_buf.shape
+    requests = q_ref.shape[0]
+    own = H // n
+    rows = own * requests
+    span = slots * own
+    others = [lax.rem(me + k, n) for k in range(1, n)]
+
+    loads = []
+    for s in range(slots):
+        load = pltpu.make_async_copy(keys_ref.at[s], key_buf.at[s], load_sem.at[s])
+        load.start()
+        loads.append(load)
+    for s in range(slots):
+        load = pltpu.make_async_copy(
+            values_ref.at[s], value_buf.at[s], load_sem.at[slots + s]
+        )
+        load.start()
+        loads.append(load)
+
+    barrier = pltpu.get_barrier_semaphore()
+    for other in others:
+        pl.semaphore_signal(
+            barrier, inc=1, device_id={"seq": other}, device_id_type=pl.DeviceIdType.MESH
+        )
+
+    mine = q_ref[...].astype(jnp.float32)
+    mine = jnp.concatenate([mine[:, c * DH : (c + 1) * DH] for c in range(own)], axis=0)
+    q_send[...] = mine.astype(jnp.bfloat16)
+    q_buf[me] = mine.astype(jnp.bfloat16)
+
+    pl.semaphore_wait(barrier, n - 1)
+
+    def send(src, dst, phase, other):
+        copy = pltpu.make_async_remote_copy(
+            src_ref=src,
+            dst_ref=dst,
+            send_sem=send_sem.at[phase],
+            recv_sem=recv_sem.at[phase],
+            device_id={"seq": other},
+            device_id_type=pl.DeviceIdType.MESH,
+        )
+        copy.start()
+
+    def drain(buf, sem):
+        pltpu.make_async_copy(buf, buf, sem).wait()
+
+    for other in others:
+        send(q_send, q_buf.at[me], 0, other)
+    half = lax.div(me, KVH)
+    head = lax.rem(me, KVH)
+    per_kv = n // KVH
+    for k in range(per_kv):
+        target = head * per_kv + k
+
+        @pl.when(target == me)
+        def _():
+            pltpu.make_async_copy(new_ref, new_buf.at[half], new_sem.at[half]).start()
+
+        @pl.when(target != me)
+        def _():
+            pltpu.make_async_remote_copy(
+                src_ref=new_ref,
+                dst_ref=new_buf.at[half],
+                send_sem=new_sem.at[2 + k],
+                recv_sem=new_sem.at[half],
+                device_id={"seq": target},
+                device_id_type=pl.DeviceIdType.MESH,
+            ).start()
+
+    others_q = q_buf.at[pl.ds(0, n - 1)]
+    drain(others_q, recv_sem.at[0])
+
+    total_rows = n * rows
+    pick_row = lax.broadcasted_iota(jnp.int32, (H, total_rows), 0)
+    pick_col = lax.broadcasted_iota(jnp.int32, (H, total_rows), 1)
+    same_head = lax.div(pick_col, requests) == pick_row
+    col_request = lax.rem(pick_col, requests)
+    everything = q_buf[...].reshape(total_rows, DH)
+    position = lax.broadcasted_iota(jnp.int32, (1, block_len), 1)
+    zero = jnp.zeros((GROUP, DH), jnp.bfloat16)
+    scale = DH ** (-0.5)
+
+    lane = lax.broadcasted_iota(jnp.int32, (GROUP, DH), 1)
+    sub = lax.broadcasted_iota(jnp.int32, (GROUP, DH), 0)
+    stat_rows = [None] * KVH
+    request_rows = [None] * KVH
+
+    picks = []
+    for s in range(slots):
+        one_hot = (same_head & (col_request == request_ref[s])).astype(jnp.bfloat16)
+        picks.append(jnp.dot(one_hot, everything, preferred_element_type=jnp.float32))
+
+    for s in range(slots):
+        loads[s].wait()
+        picked = picks[s]
+        pieces = []
+        for p in range(KVH // 2):
+            top_q = picked[2 * p * GROUP : (2 * p + 1) * GROUP].astype(jnp.bfloat16)
+            low_q = picked[(2 * p + 1) * GROUP : (2 * p + 2) * GROUP].astype(jnp.bfloat16)
+            pair = jnp.concatenate(
+                [
+                    jnp.concatenate([top_q, zero], axis=1),
+                    jnp.concatenate([zero, low_q], axis=1),
+                ],
+                axis=0,
+            )
+            pieces.append(
+                lax.dot_general(
+                    pair,
+                    key_buf[s, :, 2 * p * DH : 2 * (p + 1) * DH],
+                    (((1,), (1,)), ((), ())),
+                    preferred_element_type=jnp.float32,
+                )
+            )
+        scores = jnp.concatenate(pieces, axis=0)
+        scores = jnp.where(position < length_ref[s], scores, very_negative)
+        top = jnp.max(scores, axis=1, keepdims=True)
+        weights = jnp.exp2((scores - top) * (scale * LOG2E))
+        total = jnp.sum(weights, axis=1, keepdims=True)
+        rounded = weights.astype(jnp.bfloat16)
+        inverse = 1.0 / total
+        level = top * scale + jnp.log(total)
+        loads[slots + s].wait()
+        for p in range(KVH // 2):
+            wide = jnp.dot(
+                rounded[2 * p * GROUP : (2 * p + 2) * GROUP],
+                value_buf[s, :, 2 * p * DH : 2 * (p + 1) * DH],
+                preferred_element_type=jnp.float32,
+            )
+            for k in range(2):
+                g = 2 * p + k
+                block = wide[k * GROUP : (k + 1) * GROUP, k * DH : (k + 1) * DH]
+                block = block * inverse[g * GROUP : (g + 1) * GROUP]
+                for d in range(GROUP // own):
+                    part_send[g * (GROUP // own) + d, s * own : (s + 1) * own, :] = block[
+                        d * own : (d + 1) * own
+                    ].astype(jnp.bfloat16)
+        here = lane == me * span + s * own + lax.rem(sub, own)
+        for g in range(KVH):
+            level_g = jnp.where(here, level[g * GROUP : (g + 1) * GROUP], 0.0)
+            stat_rows[g] = level_g if s == 0 else stat_rows[g] + level_g
+        owner = jnp.where(here, request_ref[s].astype(jnp.float32), 0.0)
+        owners = owner if s == 0 else owners + owner
+
+    owners = jnp.sum(owners[:own], axis=0, keepdims=True)
+    for g in range(KVH):
+        for d in range(GROUP // own):
+            row = jnp.sum(stat_rows[g][d * own : (d + 1) * own], axis=0, keepdims=True)
+            stat_send[g * (GROUP // own) + d] = jnp.concatenate([row, owners], axis=0)
+
+    stat_buf[me] = stat_send[me]
+    part_buf[me] = part_send[me]
+    for other in others:
+        send(stat_send.at[other], stat_buf.at[me], 1, other)
+        send(part_send.at[other], part_buf.at[me], 2, other)
+
+    drain(new_buf.at[0], new_sem.at[0])
+    drain(new_buf.at[1], new_sem.at[1])
+    new_key = jnp.concatenate([new_buf[0].astype(jnp.float32)] * own, axis=0)
+    new_value = jnp.concatenate([new_buf[1].astype(jnp.float32)] * own, axis=0)
+    new_score = jnp.sum(mine * new_key, axis=1, keepdims=True) * scale
+
+    drain(stat_buf.at[pl.ds(0, n - 1)], recv_sem.at[1])
+    stats = jnp.sum(stat_buf[...], axis=0)
+    levels = stats[0:1]
+    slot_owner = stats[1:2]
+    row_id = lax.broadcasted_iota(jnp.int32, (rows, n * span), 0)
+    col_id = lax.broadcasted_iota(jnp.int32, (rows, n * span), 1)
+    same = lax.rem(col_id, own) == lax.div(row_id, requests)
+    belongs = same & (slot_owner == lax.rem(row_id, requests).astype(jnp.float32))
+    peak = jnp.max(jnp.where(belongs, levels, very_negative), axis=1, keepdims=True)
+    peak = jnp.maximum(peak, new_score)
+    mix = jnp.where(belongs, jnp.exp2((levels - peak) * LOG2E), 0.0)
+    new_weight = jnp.exp2((new_score - peak) * LOG2E)
+    denom = jnp.sum(mix, axis=1, keepdims=True) + new_weight
+    mix = mix * (1.0 / denom)
+    new_weight = new_weight * (1.0 / denom)
+    mix_high = mix.astype(jnp.bfloat16)
+    mix_low = (mix - mix_high.astype(jnp.float32)).astype(jnp.bfloat16)
+
+    drain(part_buf.at[pl.ds(0, n - 1)], recv_sem.at[2])
+    parts = part_buf[...].reshape(n * span, DH)
+    result = jnp.dot(
+        jnp.concatenate([mix_high, mix_low], axis=0), parts, preferred_element_type=jnp.float32
+    )
+    result = result[:rows] + result[rows:] + new_weight * new_value
+    result = jnp.concatenate(
+        [result[c * requests : (c + 1) * requests] for c in range(own)], axis=1
+    ).astype(jnp.bfloat16)
+    out_send[...] = result
+    columns = pl.ds(pl.multiple_of(me * own * DH, own * DH), own * DH)
+    out_ref[:, columns] = result
+    for other in others:
+        send(out_send, out_ref.at[:, columns], 3, other)
+
+    drain(q_buf.at[pl.ds(0, n - 1)], send_sem.at[0])
+    drain(stat_buf.at[pl.ds(0, n - 1)], send_sem.at[1])
+    drain(part_buf.at[pl.ds(0, n - 1)], send_sem.at[2])
+    for k in range(per_kv):
+
+        @pl.when(head * per_kv + k != me)
+        def _():
+            drain(new_buf.at[0], new_sem.at[2 + k])
+
+    rest = out_ref.at[:, pl.ds(0, (n - 1) * own * DH)]
+    drain(rest, send_sem.at[3])
+    drain(rest, recv_sem.at[3])
+
+
+def one_kernel(n, queries, new_kv, keys, values, slot_request, slot_length):
+    requests = queries.shape[0]
+    slots, block_len, width = keys.shape
+    own = H // n
+    span = slots * own
+    bf16, f32 = jnp.bfloat16, jnp.float32
+    smem = pl.BlockSpec(memory_space=pltpu.SMEM)
+    vmem = pl.BlockSpec(memory_space=pltpu.VMEM)
+    hbm = pl.BlockSpec(memory_space=pl.ANY)
+    return pl.pallas_call(
+        functools.partial(decode_kernel, n),
+        out_shape=jax.ShapeDtypeStruct((requests, H * DH), bf16),
+        in_specs=[smem, smem, vmem, vmem, hbm, hbm],
+        out_specs=vmem,
+        scratch_shapes=[
+            pltpu.VMEM((slots, block_len, width), bf16),
+            pltpu.VMEM((slots, block_len, width), bf16),
+            pltpu.VMEM((own * requests, DH), bf16),
+            pltpu.VMEM((n, own * requests, DH), bf16),
+            pltpu.VMEM((2, requests, DH), bf16),
+            pltpu.VMEM((n, span, DH), bf16),
+            pltpu.VMEM((n, span, DH), bf16),
+            pltpu.VMEM((n, 2, n * span), f32),
+            pltpu.VMEM((n, 2, n * span), f32),
+            pltpu.VMEM((requests, own * DH), bf16),
+            pltpu.SemaphoreType.DMA((2 * slots,)),
+            pltpu.SemaphoreType.DMA((2 + n // KVH,)),
+            pltpu.SemaphoreType.DMA((4,)),
+            pltpu.SemaphoreType.DMA((4,)),
+        ],
+        compiler_params=pltpu.CompilerParams(collective_id=0, has_side_effects=True),
+    )(slot_request, slot_length, queries, new_kv, keys, values)
 
 
 def joined(x, axis, combine):
@@ -32,7 +306,7 @@
     return (peak, summed, outputs)
 
 
-def shards(queries, new_kv, keys, values, slot_request, slot_length):
+def gathered(queries, new_kv, keys, values, slot_request, slot_length):
     all_queries, all_new = (
         lax.all_gather(queries, "seq", axis=1, tiled=True),
         lax.all_gather(new_kv, "seq", axis=1, tiled=True),
@@ -88,6 +362,13 @@
     return attended.reshape(requests, H * DH).astype(jnp.bfloat16)
 
 
+def shards(n, queries, new_kv, keys, values, slot_request, slot_length):
+    whole_heads = n == 2 * KVH and n * keys.shape[0] * (H // n) == DH
+    if whole_heads:
+        return one_kernel(n, queries, new_kv, keys, values, slot_request, slot_length)
+    return gathered(queries, new_kv, keys, values, slot_request, slot_length)
+
+
 def solution(mesh):
     placed = (
         P("parts", "seq"),
@@ -98,5 +379,9 @@
         P(("parts", "seq")),
     )
     return jax.shard_map(
-        shards, mesh=mesh, in_specs=placed, out_specs=P("parts", None), check_vma=False
-    )
+        functools.partial(shards, mesh.shape["seq"]),
+        mesh=mesh,
+        in_specs=placed,
+        out_specs=P("parts", None),
+        check_vma=False,
+    )

time: 120 us -> 22.3 us (0.19)
  blocking collectives: 79.2 us -> 0 us
  Pallas kernels: 0 us -> 20.6 us
  other arithmetic: 18.8 us -> 0 us
  between operations: 13.5 us -> 0.01 us
  matrix products: 4.7 us -> 0 us
  local copies, waits for them, and re-layouts: 2.76 us -> 1.49 us
    all_gather x4 -> x0, blocking collectives: 79.2 us -> none  [the longest x2 38.2 us: joined(): everything = jax.tree.map(lambda part: lax.all_gather(part, axis), x)]
    pallas_call x0 -> x1, Pallas kernels: none -> 20.6 us  [one_kernel(): pl.pallas_call(functools.partial(decode_kernel, n), out_shape=jax.ShapeDt...]
    add x30 -> x0, other arithmetic: 16.4 us -> none  [the longest x15 16.1 us: combine_parts(): out_first * weight_first[..., None] + out_second * weight_second[..., None]]
    dot_general x5 -> x0, matrix products: 4.7 us -> none  [the longest x1 2.06 us: shards(): jnp.einsum('skgt,stkd->skgd', weights.astype(jnp.bfloat16), value_tiles,...]
  transfers between devices with their start and end apart: 1 -> 0, of which waited for: 0 -> 0; matrix products, arithmetic and copies ran while one was open for 1% -> 0% of each run, Pallas kernels for 0% -> 0%
where the time goes in v1:
time: 22.3 us; the launch traced here: 22.1 us
  Pallas kernels  20.6 us (92%)
  local copies, waits for them, and re-layouts  1.49 us (7%)
    pallas_call x1, Pallas kernels, one_kernel(): pl.pallas_call(functools.partial(decode_kernel, n), out_shape=jax.ShapeDt...  20.6 us
    unnamed x1, local copies, waits for them, and re-layouts  1.49 us

profile of v1, /device:TPU:0, one launch (start us, length us, event | category | flops | bytes accessed | tf_op | source)
XLA Modules:
  0.0 22.1 jit_solution(5392055006081388107)
XLA Ops:
  0.0 20.6 %shard_map.64 = bf16[4,8192]{1,0:T(4,128)(2,1)} custom-call(s32[2]{0:T(128)} %request_ref.1, s32[2]{0:T(128)} %length_ref.1, bf16[4,512]{1,0:T(4,128)(2,1)} %q_ref.1, bf16[4,128]{1,0:T(4,128)(2,1)} %new_ref.1, bf16[2,512,1024]{2,1,0:T(8,128)(2,1)} %keys_ref.1, bf16[2,512,1024]{2,1,0:T(8,128)(2,1)} %values_ref.1), custom_call_target="tpu_custom_call" | custom-call | tf_op jit(solution)/shard_map/pallas_call | solution.py:263
  20.6 1.5 %copy.8 = bf16[4,8192]{1,0:T(4,128)(2,1)} copy(bf16[4,8192]{1,0:T(4,128)(2,1)} %shard_map.64) | data formatting | bytes 131072

commit v2 on v1

--- a/solution.py
+++ b/solution.py
@@ -19,13 +19,18 @@
 
 def decode_kernel(
     n,
-    request_ref,
-    length_ref,
-    q_ref,
-    new_ref,
+    request_hbm,
+    length_hbm,
+    q_hbm,
+    new_hbm,
     keys_ref,
     values_ref,
     out_ref,
+    q_ref,
+    new_ref,
+    request_ref,
+    length_ref,
+    small_sem,
     key_buf,
     value_buf,
     q_send,
@@ -49,6 +54,19 @@
     span = slots * own
     others = [lax.rem(me + k, n) for k in range(1, n)]
 
+    barrier = pltpu.get_barrier_semaphore()
+    for other in others:
+        pl.semaphore_signal(
+            barrier, inc=1, device_id={"seq": other}, device_id_type=pl.DeviceIdType.MESH
+        )
+
+    small = []
+    for k, (src, dst) in enumerate(
+        [(q_hbm, q_ref), (new_hbm, new_ref), (request_hbm, request_ref), (length_hbm, length_ref)]
+    ):
+        copy = pltpu.make_async_copy(src, dst, small_sem.at[k])
+        copy.start()
+        small.append(copy)
     loads = []
     for s in range(slots):
         load = pltpu.make_async_copy(keys_ref.at[s], key_buf.at[s], load_sem.at[s])
@@ -61,12 +79,7 @@
         load.start()
         loads.append(load)
 
-    barrier = pltpu.get_barrier_semaphore()
-    for other in others:
-        pl.semaphore_signal(
-            barrier, inc=1, device_id={"seq": other}, device_id_type=pl.DeviceIdType.MESH
-        )
-
+    small[0].wait()
     mine = q_ref[...].astype(jnp.float32)
     mine = jnp.concatenate([mine[:, c * DH : (c + 1) * DH] for c in range(own)], axis=0)
     q_send[...] = mine.astype(jnp.bfloat16)
@@ -90,6 +103,8 @@
 
     for other in others:
         send(q_send, q_buf.at[me], 0, other)
+    for copy in small[1:]:
+        copy.wait()
     half = lax.div(me, KVH)
     head = lax.rem(me, KVH)
     per_kv = n // KVH
@@ -257,15 +272,19 @@
     own = H // n
     span = slots * own
     bf16, f32 = jnp.bfloat16, jnp.float32
-    smem = pl.BlockSpec(memory_space=pltpu.SMEM)
     vmem = pl.BlockSpec(memory_space=pltpu.VMEM)
     hbm = pl.BlockSpec(memory_space=pl.ANY)
     return pl.pallas_call(
         functools.partial(decode_kernel, n),
         out_shape=jax.ShapeDtypeStruct((requests, H * DH), bf16),
-        in_specs=[smem, smem, vmem, vmem, hbm, hbm],
+        in_specs=[hbm] * 6,
         out_specs=vmem,
         scratch_shapes=[
+            pltpu.VMEM(queries.shape, bf16),
+            pltpu.VMEM(new_kv.shape, bf16),
+            pltpu.SMEM(slot_request.shape, jnp.int32),
+            pltpu.SMEM(slot_length.shape, jnp.int32),
+            pltpu.SemaphoreType.DMA((4,)),
             pltpu.VMEM((slots, block_len, width), bf16),
             pltpu.VMEM((slots, block_len, width), bf16),
             pltpu.VMEM((own * requests, DH), bf16),

time: 22.3 us -> 21.5 us (0.964)
  Pallas kernels: 20.6 us -> 19.9 us
    pallas_call x1, Pallas kernels: 20.6 us -> 19.9 us  [one_kernel(): pl.pallas_call(functools.partial(decode_kernel, n), out_shape=jax.ShapeDt...]
where the time goes in v2:
time: 21.5 us; the launch traced here: 21.4 us
  Pallas kernels  19.9 us (93%)
  local copies, waits for them, and re-layouts  1.49 us (7%)
    pallas_call x1, Pallas kernels, one_kernel(): pl.pallas_call(functools.partial(decode_kernel, n), out_shape=jax.ShapeDt...  19.9 us
    unnamed x1, local copies, waits for them, and re-layouts  1.49 us

profile of v2, /device:TPU:0, one launch (start us, length us, event | category | flops | bytes accessed | tf_op | source)
XLA Modules:
  0.0 21.4 jit_solution(7738665707696176843)
XLA Ops:
  0.0 19.9 %shard_map.64 = bf16[4,8192]{1,0:T(4,128)(2,1)} custom-call(s32[2]{0:T(128)} %request_hbm.1, s32[2]{0:T(128)} %length_hbm.1, bf16[4,512]{1,0:T(4,128)(2,1)} %q_hbm.1, bf16[4,128]{1,0:T(4,128)(2,1)} %new_hbm.1, bf16[2,512,1024]{2,1,0:T(8,128)(2,1)} %keys_ref.1, bf16[2,512,1024]{2,1,0:T(8,128)(2,1)} %values_ref.1), custom_call_target="tpu_custom_call" | custom-call | tf_op jit(solution)/shard_map/pallas_call | solution.py:277
  19.9 1.5 %copy.8 = bf16[4,8192]{1,0:T(4,128)(2,1)} copy(bf16[4,8192]{1,0:T(4,128)(2,1)} %shard_map.64) | data formatting | bytes 131072

commit v3 on v2

--- a/solution.py
+++ b/solution.py
@@ -276,7 +276,7 @@
     hbm = pl.BlockSpec(memory_space=pl.ANY)
     return pl.pallas_call(
         functools.partial(decode_kernel, n),
-        out_shape=jax.ShapeDtypeStruct((requests, H * DH), bf16),
+        out_shape=pltpu.VMEM((requests, H * DH), bf16),
         in_specs=[hbm] * 6,
         out_specs=vmem,
         scratch_shapes=[

time: 21.5 us -> 20 us (0.930)
  local copies, waits for them, and re-layouts: 1.49 us -> 0.63 us
  Pallas kernels: 19.9 us -> 19.2 us
    unnamed x1, local copies, waits for them, and re-layouts: 1.49 us -> 0.63 us
    pallas_call x1, Pallas kernels: 19.9 us -> 19.2 us  [one_kernel(): pl.pallas_call(functools.partial(decode_kernel, n), out_shape=pltpu.VMEM(...]
where the time goes in v3:
time: 20 us; the launch traced here: 19.9 us
  Pallas kernels  19.2 us (96%)
  local copies, waits for them, and re-layouts  0.63 us (3%)
    pallas_call x1, Pallas kernels, one_kernel(): pl.pallas_call(functools.partial(decode_kernel, n), out_shape=pltpu.VMEM(...  19.2 us
    unnamed x1, local copies, waits for them, and re-layouts  0.63 us

profile of v3, /device:TPU:0, one launch (start us, length us, event | category | flops | bytes accessed | tf_op | source)
XLA Modules:
  0.0 19.9 jit_solution(4543991420868212256)
XLA Ops:
  0.0 19.2 %shard_map.64 = bf16[4,8192]{1,0:T(4,128)(2,1)S(1)} custom-call(s32[2]{0:T(128)} %request_hbm.1, s32[2]{0:T(128)} %length_hbm.1, bf16[4,512]{1,0:T(4,128)(2,1)} %q_hbm.1, bf16[4,128]{1,0:T(4,128)(2,1)} %new_hbm.1, bf16[2,512,1024]{2,1,0:T(8,128)(2,1)} %keys_ref.1, bf16[2,512,1024]{2,1,0:T(8,128)(2,1)} %values_ref.1), custom_call_target="tpu_custom_call" | custom-call | tf_op jit(solution)/shard_map/pallas_call | solution.py:277
  19.2 0.6 %copy.8 = bf16[4,8192]{1,0:T(4,128)(2,1)} copy(bf16[4,8192]{1,0:T(4,128)(2,1)S(1)} %shard_map.64) | data formatting | bytes 131072
